TPU v7x, 32 devices: a whole 2x2x4 slice. The times are simulated.
32 devices in a mesh: groups: 2 (over x), dp: 2 (over core), seq: 8 (over z, y).
Axes of the slice: x: 2, y: 2, z: 4, core: 2. Of those that a mesh axis runs over, the one named last changes fastest.
Arguments:
- history: bfloat16 [8, 768, 1024], P(('groups', 'dp'), 'seq'), parts along dimension 0, may hold values from -20 to 20
- candidates: bfloat16 [4, 512, 1024], P(('groups', 'dp'), 'seq'), parts along dimension 0, may hold values from -6 to 6
- lengths: int32 [8], P(('groups', 'dp')), parts along dimension 0, may hold values from 96 to 768
- assignment: int32 [4, 512], P(('groups', 'dp'), 'seq'), parts along dimension 0, may hold values from 0 to 1, as said below
- weight_in: bfloat16 [1024, 4096], replicated, may hold values from -0.1875 to 0.1875
- weight_out: bfloat16 [1024, 1024], replicated, may hold values from -0.1875 to 0.1875
- gain_in: float32 [1024], replicated, may hold values from 0.25 to 1.75
- gain_attn: float32 [1024], replicated, may hold values from 0.25 to 1.75
Outputs:
- history_out: bfloat16 [8, 768, 1024], P(('groups', 'dp'), 'seq'), parts along dimension 0
- candidate_out: bfloat16 [4, 512, 1024], P(('groups', 'dp'), 'seq'), parts along dimension 0
There are 2 independent parts, one for each index of `groups`. A program takes and returns all parts, laid end to end along the dimension named above; an argument that names none is the same for every part. Nothing has to cross between parts.
Inputs may be any that keep to these rules, and one draw needn't show every extreme that they name: `assignment`: of the 64 candidates of one device, at most 40 belong to either history; in every dp index some device has exactly 40 of the first and another exactly 40 of the second.
All inputs are finite; a program needn't handle non-finite values.
Results may differ from a plain program's by a relative error of at most 0.0075.
Values may be sent and summed in bfloat16 or wider, within the bound.
A program may use at most 192 MiB of HBM per device.

v0:
```python
import math
import jax
import jax.numpy as jnp
from jax import lax
from jax.sharding import PartitionSpec as P

H = 16
HD = 64
CAP = 40


def rms_apply(values, gain):
    return values * lax.rsqrt(jnp.mean(values * values, axis=-1, keepdims=True) + 1e-06) * gain


def self_item(packed):
    query, keys, values, valid = packed
    length = keys.shape[0]
    score_scale = HD ** (-0.5)
    block_rows = math.gcd(length, 512)
    key_positions = jnp.arange(length, dtype=jnp.int32)

    def query_part(inner):
        query_block, first_row = inner
        scores = jnp.dot(query_block, keys.T, preferred_element_type=jnp.float32) * score_scale
        row_positions = first_row + jnp.arange(block_rows, dtype=jnp.int32)
        allowed = (key_positions[None, :] <= row_positions[:, None]) & (
            key_positions[None, :] < valid
        )
        weights = jnp.where(allowed, jax.nn.silu(scores), 0.0).astype(jnp.bfloat16)
        return jnp.dot(weights, values, preferred_element_type=jnp.float32).astype(jnp.bfloat16)

    starts = jnp.arange(length // block_rows, dtype=jnp.int32) * block_rows
    result = lax.map(query_part, (query.reshape(length // block_rows, block_rows, HD), starts))
    return result.reshape(length, HD)


def cand_item(packed):
    queries, keys, values, valid = packed
    cand_total = queries.shape[0]
    score_scale = HD ** (-0.5)
    block_rows = math.gcd(cand_total, 1024)
    key_positions = jnp.arange(keys.shape[0], dtype=jnp.int32)

    def cand_part(query_block):
        scores = jnp.dot(query_block, keys.T, preferred_element_type=jnp.float32) * score_scale
        weights = jnp.where(key_positions[None, :] < valid, jax.nn.silu(scores), 0.0).astype(
            jnp.bfloat16
        )
        return jnp.dot(weights, values, preferred_element_type=jnp.float32).astype(jnp.bfloat16)

    result = lax.map(cand_part, queries.reshape(cand_total // block_rows, block_rows, HD))
    return result.reshape(cand_total, HD)


def place_windows(windows, cand_count, window_rows, inverse):
    first = jnp.pad(windows[0], ((0, cand_count - window_rows), (0, 0), (0, 0)))
    second = jnp.pad(windows[1], ((cand_count - window_rows, 0), (0, 0), (0, 0)))
    return (first + second)[inverse]


def per_device(history, candidates, lengths, assignment, weight_in, weight_out, gain_in, gain_attn):
    seq_devices = lax.axis_size("seq")
    hist_local, tok_share, model_width = history.shape
    item_count = hist_local * H
    items_local = item_count // seq_devices
    length = tok_share * seq_devices
    hist_float = history.astype(jnp.float32)
    normed = (
        rms_apply(hist_float, gain_in)
        .astype(jnp.bfloat16)
        .reshape(hist_local * tok_share, model_width)
    )
    projected = jnp.dot(normed, weight_in, preferred_element_type=jnp.float32)
    gate = jax.nn.silu(projected[:, :model_width]).astype(jnp.bfloat16)
    query = projected[:, model_width : 2 * model_width].astype(jnp.bfloat16)
    keys = projected[:, 2 * model_width : 3 * model_width].astype(jnp.bfloat16)
    values = projected[:, 3 * model_width :].astype(jnp.bfloat16)

    def to_items(matrix):
        return (
            matrix.reshape(hist_local, tok_share, H, HD)
            .transpose(0, 2, 1, 3)
            .reshape(item_count, tok_share * HD)
        )

    exchanged = (
        lax.all_to_all(to_items(query), "seq", split_axis=0, concat_axis=1, tiled=True),
        lax.all_to_all(to_items(keys), "seq", split_axis=0, concat_axis=1, tiled=True),
        lax.all_to_all(to_items(values), "seq", split_axis=0, concat_axis=1, tiled=True),
    )
    heads_query = exchanged[0].reshape(items_local, length, HD)
    heads_keys = exchanged[1].reshape(items_local, length, HD)
    heads_values = exchanged[2].reshape(items_local, length, HD)
    first_item = lax.axis_index("seq") * items_local
    item_hist = (first_item + jnp.arange(items_local, dtype=jnp.int32)) // H
    members = jnp.arange(hist_local, dtype=jnp.int32)
    item_valid = jnp.sum(
        jnp.where(item_hist[:, None] == members[None, :], lengths[None, :], 0), axis=1
    )
    attended = lax.map(self_item, (heads_query, heads_keys, heads_values, item_valid))
    returned = lax.all_to_all(
        attended.reshape(items_local, length * HD), "seq", split_axis=1, concat_axis=0, tiled=True
    )
    returned = (
        returned.reshape(hist_local, H, tok_share, HD)
        .transpose(0, 2, 1, 3)
        .reshape(hist_local * tok_share, model_width)
    )
    gated_rows = (
        rms_apply(returned.astype(jnp.float32), gain_attn) * gate.astype(jnp.float32)
    ).astype(jnp.bfloat16)
    history_out = hist_float.reshape(hist_local * tok_share, model_width) + jnp.dot(
        gated_rows, weight_out, preferred_element_type=jnp.float32
    )
    history_out = history_out.astype(jnp.bfloat16).reshape(hist_local, tok_share, model_width)
    cand_rows = candidates[0]
    cand_count = cand_rows.shape[0]
    window_rows = CAP
    owner = assignment[0]
    cand_float = cand_rows.astype(jnp.float32)
    cand_normed = rms_apply(cand_float, gain_in).astype(jnp.bfloat16)
    cand_proj = jnp.dot(
        cand_normed, weight_in[:, : 2 * model_width], preferred_element_type=jnp.float32
    )
    cand_gate = jax.nn.silu(cand_proj[:, :model_width]).astype(jnp.bfloat16)
    cand_query = cand_proj[:, model_width:].astype(jnp.bfloat16).reshape(cand_count, H, HD)
    order = jnp.argsort(owner * cand_count + jnp.arange(cand_count, dtype=jnp.int32))
    inverse = jnp.argsort(order)
    sorted_query = cand_query[order]
    sorted_owner = owner[order]
    window_starts = [0, cand_count - window_rows]
    window_list = []
    for member in range(hist_local):
        start = window_starts[member]
        rows_here = sorted_query[start : start + window_rows]
        mine = sorted_owner[start : start + window_rows] == member
        window_list.append(jnp.where(mine[:, None, None], rows_here, jnp.zeros_like(rows_here)))
    window_query = jnp.stack(window_list)
    outgoing = window_query.transpose(0, 2, 1, 3).reshape(item_count, window_rows * HD)
    incoming = lax.all_to_all(outgoing, "seq", split_axis=0, concat_axis=1, tiled=True)
    incoming = incoming.reshape(items_local, seq_devices * window_rows, HD)
    results = lax.map(cand_item, (incoming, heads_keys, heads_values, item_valid))
    back_home = lax.all_to_all(
        results.reshape(items_local, seq_devices * window_rows * HD),
        "seq",
        split_axis=1,
        concat_axis=0,
        tiled=True,
    )
    back_home = (
        back_home.reshape(hist_local, H, window_rows, HD).transpose(0, 2, 1, 3).astype(jnp.float32)
    )
    cross_attended = (
        place_windows(back_home, cand_count, window_rows, inverse)
        .astype(jnp.bfloat16)
        .reshape(cand_count, model_width)
    )
    cand_gated = (
        rms_apply(cross_attended.astype(jnp.float32), gain_attn) * cand_gate.astype(jnp.float32)
    ).astype(jnp.bfloat16)
    candidate_out = (
        cand_float + jnp.dot(cand_gated, weight_out, preferred_element_type=jnp.float32)
    ).astype(jnp.bfloat16)
    return (history_out, candidate_out[None])


def solution(mesh):
    in_specs = (
        P(("groups", "dp"), "seq", None),
        P(("groups", "dp"), "seq", None),
        P(("groups", "dp")),
        P(("groups", "dp"), "seq"),
        P(),
        P(),
        P(),
        P(),
    )
    out_specs = (P(("groups", "dp"), "seq", None), P(("groups", "dp"), "seq", None))
    return jax.shard_map(
        per_device, mesh=mesh, in_specs=in_specs, out_specs=out_specs, check_vma=False
    )
```

profile of v0, /device:TPU:0, one launch (start us, length us, event | category | flops | bytes accessed | tf_op | source)
XLA Modules:
  0.0 198.5 jit_solution(17433720871256379200)
XLA Ops:
  1.5 2.0 %sort.31 = (s32[64]{0:T(128)}, s32[64]{0:T(128)S(1)}) sort(s32[64]{0:T(128)S(1)} %iota_add_fusion.1, s32[64]{0:T(128)S(1)} %iota.37), dimensions={0}, to_apply=%region_8.9 | sort | flops 384 | bytes 1024 | tf_op jit(solution)/shard_map/jit(argsort)/sort | solution.py:128
  4.6 3.2 %fusion.37 = f32[64,2048]{1,0:T(8,128)S(1)} fusion(bf16[1024,4096]{1,0:T(8,128)(2,1)} %param.20, bf16[1,64,1024]{2,1,0:T(8,128)(2,1)} %param.17, f32[1024]{0:T(1024)} %param.22, f32[64]{0:T(128)S(1)} %add_rsqrt_fusion.3), kind=kOutput, calls=%fused_computation.50 | convolution fusion | flops 268697600 | bytes 4854016 | tf_op jit(solution)/shard_map/dot_general | solution.py:123
  11.5 7.3 %all-to-all-start.4 = ((bf16[8,4,2560]{2,1,0:T(4,128)(2,1)}), bf16[8,4,2560]{2,1,0:T(4,128)(2,1)}, u32[]{:S(2)}, u32[]{:S(2)}) async-start(bf16[8,4,2560]{2,1,0:T(4,128)(2,1)} %all_to_all.79), calls=%async_computation.4 | async-start | bytes 327680 | tf_op jit(solution)/shard_map/all_to_all | solution.py:141
  19.1 6.9 %fusion.62 = (bf16[192,4096]{1,0:T(8,128)(2,1)S(1)}, f32[192,4096]{1,0:T(8,128)}) fusion(bf16[192,1024]{1,0:T(8,128)(2,1)S(1)} %bitcast.139, bf16[1024,4096]{1,0:T(8,128)(2,1)} %param.20), kind=kOutput, calls=%fused_computation.113 | convolution fusion | flops 1611399168 | bytes 13500416 | tf_op jit(solution)/shard_map/dot_general | solution.py:74
  28.1 1.3 all_to_all.71
  29.4 6.0 %all-to-all-start.1 = ((bf16[8,4,6144]{2,1,0:T(4,128)(2,1)}), bf16[8,4,6144]{2,1,0:T(4,128)(2,1)}, u32[]{:S(2)}, u32[]{:S(2)}) async-start(bf16[8,4,6144]{2,1,0:T(4,128)(2,1)} %all_to_all.71), calls=%async_computation.1 | async-start | bytes 786432 | tf_op jit(solution)/shard_map/all_to_all | solution.py:89
  37.4 1.3 all_to_all.74
  38.7 7.8 %all-to-all-done.1 = bf16[8,4,6144]{2,1,0:T(4,128)(2,1)} async-done(((bf16[8,4,6144]{2,1,0:T(4,128)(2,1)}), bf16[8,4,6144]{2,1,0:T(4,128)(2,1)}, u32[]{:S(2)}, u32[]{:S(2)}) %all-to-all-start.1) | async-done | bytes 393248 | tf_op jit(solution)/shard_map/all_to_all | solution.py:89
  46.6 4.1 %all-to-all-start.2 = ((bf16[8,4,6144]{2,1,0:T(4,128)(2,1)}), bf16[8,4,6144]{2,1,0:T(4,128)(2,1)}, u32[]{:S(2)}, u32[]{:S(2)}) async-start(bf16[8,4,6144]{2,1,0:T(4,128)(2,1)} %all_to_all.74), calls=%async_computation.2 | async-start | bytes 786432 | tf_op jit(solution)/shard_map/all_to_all | solution.py:90
  50.7 2.0 %sort.32 = (s32[64]{0:T(128)}, s32[64]{0:T(128)S(1)}) sort(s32[64]{0:T(128)S(1)} %get-tuple-element.151, s32[64]{0:T(128)S(1)} %iota.38), dimensions={0}, to_apply=%region_14.15 | sort | flops 384 | bytes 1024 | tf_op jit(solution)/shard_map/jit(argsort)/sort | solution.py:129
  54.8 1.3 all_to_all.68
  58.1 1.2 copy.67
  60.1 1.7 all-to-all-done.2
  61.9 4.2 %all-to-all-start = ((bf16[8,4,6144]{2,1,0:T(4,128)(2,1)}), bf16[8,4,6144]{2,1,0:T(4,128)(2,1)}, u32[]{:S(2)}, u32[]{:S(2)}) async-start(bf16[8,4,6144]{2,1,0:T(4,128)(2,1)} %all_to_all.68), calls=%async_computation | async-start | bytes 786432 | tf_op jit(solution)/shard_map/all_to_all | solution.py:88
  67.3 1.7 reshape.190
  68.9 32.8 %while.46 = (s32[]{:T(128)}, bf16[4,320,64]{2,1,0:T(8,128)(2,1)}, bf16[4,320,64]{2,1,0:T(8,128)(2,1)}, bf16[4,768,64]{2,1,0:T(8,128)(2,1)S(1)}, s32[4]{0:T(128)S...) while((s32[]{:T(128)}, bf16[4,320,64]{2,1,0:T(8,128)(2,1)}, ...), condition=%wide.region_13.14_spmd, body=%wide.region_10.13_spmd.sunk | while | flops 12931844 | bytes 1027586 | solution.py:143
  71.4 5.1 %while.48 = (s32[]{:T(128)}, bf16[5,64,64]{2,1,0:T(8,128)(2,1)S(1)}, s32[]{:T(128)}, bf16[5,64,64]{2,1,0:T(8,128)(2,1)S(1)}, bf16[768,64]{1,0:T(8,128)(2,1)S(1)}, /*index=5*/bf16[768,64]{1,0:T(8,128)(2,1)S(1)}, s32[]{:T(128)}) while((s32[]{:T(128)}, bf16[5,64,64]{2,1,0:T(8,128)(2,1)S(1)}, s32[]{:T(128)}, ...), condition=%wide.region_12.12_spmd.clone, body=%wide.region_11.11_spmd.clone.sunk | while | flops 12931842 | bytes 428881 | solution.py:52
  79.6 5.1 %while.48 = (s32[]{:T(128)}, bf16[5,64,64]{2,1,0:T(8,128)(2,1)S(1)}, s32[]{:T(128)}, bf16[5,64,64]{2,1,0:T(8,128)(2,1)S(1)}, bf16[768,64]{1,0:T(8,128)(2,1)S(1)}, /*index=5*/bf16[768,64]{1,0:T(8,128)(2,1)S(1)}, s32[]{:T(128)}) while((s32[]{:T(128)}, bf16[5,64,64]{2,1,0:T(8,128)(2,1)S(1)}, s32[]{:T(128)}, ...), condition=%wide.region_12.12_spmd.clone, body=%wide.region_11.11_spmd.clone.sunk | while | flops 12931842 | bytes 428881 | solution.py:52
  87.8 5.1 %while.48 = (s32[]{:T(128)}, bf16[5,64,64]{2,1,0:T(8,128)(2,1)S(1)}, s32[]{:T(128)}, bf16[5,64,64]{2,1,0:T(8,128)(2,1)S(1)}, bf16[768,64]{1,0:T(8,128)(2,1)S(1)}, /*index=5*/bf16[768,64]{1,0:T(8,128)(2,1)S(1)}, s32[]{:T(128)}) while((s32[]{:T(128)}, bf16[5,64,64]{2,1,0:T(8,128)(2,1)S(1)}, s32[]{:T(128)}, ...), condition=%wide.region_12.12_spmd.clone, body=%wide.region_11.11_spmd.clone.sunk | while | flops 12931842 | bytes 428881 | solution.py:52
  96.0 5.1 %while.48 = (s32[]{:T(128)}, bf16[5,64,64]{2,1,0:T(8,128)(2,1)S(1)}, s32[]{:T(128)}, bf16[5,64,64]{2,1,0:T(8,128)(2,1)S(1)}, bf16[768,64]{1,0:T(8,128)(2,1)S(1)}, /*index=5*/bf16[768,64]{1,0:T(8,128)(2,1)S(1)}, s32[]{:T(128)}) while((s32[]{:T(128)}, bf16[5,64,64]{2,1,0:T(8,128)(2,1)S(1)}, s32[]{:T(128)}, ...), condition=%wide.region_12.12_spmd.clone, body=%wide.region_11.11_spmd.clone.sunk | while | flops 12931842 | bytes 428881 | solution.py:52
  101.7 1.2 all_to_all.82
  103.7 6.0 %all-to-all-start.5 = ((bf16[4,8,2560]{2,0,1:T(4,128)(2,1)}), bf16[4,8,2560]{2,0,1:T(4,128)(2,1)}, u32[]{:S(2)}, u32[]{:S(2)}) async-start(bf16[4,8,2560]{2,0,1:T(4,128)(2,1)} %copy.76), calls=%async_computation.5 | async-start | bytes 327680 | tf_op jit(solution)/shard_map/all_to_all | solution.py:144
  110.9 1.7 reshape.186
  112.6 55.4 %while.44 = (s32[]{:T(128)}, bf16[4,768,64]{2,1,0:T(8,128)(2,1)}, bf16[4,768,64]{2,1,0:T(8,128)(2,1)}, bf16[4,768,64]{2,1,0:T(8,128)(2,1)S(1)}, s32[4]{0:T(128)S...) while((s32[]{:T(128)}, bf16[4,768,64]{2,1,0:T(8,128)(2,1)}, ...), condition=%wide.region_5.6_spmd, body=%wide.region_2.5_spmd.sunk | while | flops 52118532 | bytes 1578542 | solution.py:101
  115.1 9.6 %while.47 = (s32[]{:T(128)}, bf16[3,256,64]{1,2,0:T(8,128)(2,1)}, s32[3]{0:T(128)S(1)}, s32[]{:T(128)}, bf16[3,256,64]{2,1,0:T(8,128)(2,1)S(1)}, /*index=5*/bf16...) while((s32[]{:T(128)}, bf16[3,256,64]{1,2,0:T(8,128)(2,1)}, ...), condition=%wide.region_4.4_spmd.clone.clone, body=%wide.region_3.3_spmd.clone.clone.sunk | while | flops 52118528 | bytes 496489 | solution.py:34
  117.0 1.3 fusion.86
  120.2 1.3 fusion.86
  123.4 1.3 fusion.86
  128.9 9.6 %while.47 = (s32[]{:T(128)}, bf16[3,256,64]{1,2,0:T(8,128)(2,1)}, s32[3]{0:T(128)S(1)}, s32[]{:T(128)}, bf16[3,256,64]{2,1,0:T(8,128)(2,1)S(1)}, /*index=5*/bf16...) while((s32[]{:T(128)}, bf16[3,256,64]{1,2,0:T(8,128)(2,1)}, ...), condition=%wide.region_4.4_spmd.clone.clone, body=%wide.region_3.3_spmd.clone.clone.sunk | while | flops 52118528 | bytes 496489 | solution.py:34
  130.9 1.3 fusion.86
  134.1 1.3 fusion.86
  137.3 1.3 fusion.86
  142.8 9.6 %while.47 = (s32[]{:T(128)}, bf16[3,256,64]{1,2,0:T(8,128)(2,1)}, s32[3]{0:T(128)S(1)}, s32[]{:T(128)}, bf16[3,256,64]{2,1,0:T(8,128)(2,1)S(1)}, /*index=5*/bf16...) while((s32[]{:T(128)}, bf16[3,256,64]{1,2,0:T(8,128)(2,1)}, ...), condition=%wide.region_4.4_spmd.clone.clone, body=%wide.region_3.3_spmd.clone.clone.sunk | while | flops 52118528 | bytes 496489 | solution.py:34
  144.7 1.3 fusion.86
  147.9 1.3 fusion.86
  151.1 1.3 fusion.86
  156.6 9.6 %while.47 = (s32[]{:T(128)}, bf16[3,256,64]{1,2,0:T(8,128)(2,1)}, s32[3]{0:T(128)S(1)}, s32[]{:T(128)}, bf16[3,256,64]{2,1,0:T(8,128)(2,1)S(1)}, /*index=5*/bf16...) while((s32[]{:T(128)}, bf16[3,256,64]{1,2,0:T(8,128)(2,1)}, ...), condition=%wide.region_4.4_spmd.clone.clone, body=%wide.region_3.3_spmd.clone.clone.sunk | while | flops 52118528 | bytes 496489 | solution.py:34
  158.6 1.3 fusion.86
  161.8 1.3 fusion.86
  165.0 1.3 fusion.86
  168.0 1.8 all_to_all.77
  170.8 6.0 %all-to-all-start.3 = ((bf16[4,8,6144]{2,0,1:T(4,128)(2,1)}), bf16[4,8,6144]{2,0,1:T(4,128)(2,1)S(1)}, u32[]{:S(2)}, u32[]{:S(2)}) async-start(bf16[4,8,6144]{2,0,1:T(4,128)(2,1)} %copy.71), calls=%async_computation.3 | async-start | bytes 786432 | tf_op jit(solution)/shard_map/all_to_all | solution.py:102
  179.7 2.1 %fusion.41 = bf16[1,64,1024]{2,1,0:T(8,128)(2,1)} fusion(bf16[1024,1024]{1,0:T(8,128)(2,1)S(1)} %copy-done, f32[64,1024]{1,0:T(8,128)S(1)} %reshape.196, f32[64,2048]{1,0:T(8,128)} %copy-done.5, bf16[1,64,1024]{2,1,0:T(8,128)(2,1)S(1)} %copy-done.4, f32[1024]{0:T(1024)S(1)} %copy-done.7, f32[64]{0:T(128)S(1)} %add_rsqrt_fusion.2), kind=kOutput, calls=%fused_computation.56 | convolution fusion | flops 135069696 | bytes 2887936 | tf_op jit(solution)/shard_map/dot_general | solution.py:163
  181.8 4.8 %all-to-all-done.3 = bf16[4,8,6144]{2,0,1:T(4,128)(2,1)S(1)} async-done(((bf16[4,8,6144]{2,0,1:T(4,128)(2,1)}), bf16[4,8,6144]{2,0,1:T(4,128)(2,1)S(1)}, u32[]{:S(2)}, u32[]{:S(2)}) %all-to-all-start.3) | async-done | bytes 393248 | tf_op jit(solution)/shard_map/all_to_all | solution.py:102
  186.7 1.9 reshape.198
  188.6 3.5 %copy.78 = f32[2,96,16,64]{3,2,1,0:T(8,128)} copy(f32[2,96,16,64]{3,1,2,0:T(8,128)} %bitcast.136) | data formatting | bytes 1572864 | tf_op jit(solution)/shard_map/convert_element_type | solution.py:111
  192.1 2.7 %reshape.226 = f32[192,1024]{1,0:T(8,128)} reshape(f32[2,96,16,64]{3,2,1,0:T(8,128)} %copy.78) | data formatting | bytes 1572864 | tf_op jit(solution)/shard_map/convert_element_type | solution.py:111
  195.7 2.8 %fusion.39 = bf16[192,1024]{1,0:T(8,128)(2,1)} fusion(bf16[1024,1024]{1,0:T(8,128)(2,1)S(1)} %copy-done, f32[192,1024]{1,0:T(8,128)} %reshape.226, f32[192,4096]{1,0:T(8,128)} %get-tuple-element.268, f32[1024]{0:T(1024)S(1)} %copy-done.7, f32[192]{0:T(256)S(1)} %rsqrt.37, bf16[192,1024]{1,0:T(8,128)(2,1)S(1)} %bitcast.145), kind=kOutput, calls=%fused_computation.53 | convolution fusion | flops 405209088 | bytes 4461312 | tf_op jit(solution)/shard_map/dot_general | solution.py:113
  (202 shorter events, 95.1 us)
Async XLA Ops:
  0.6 179.1 %copy-start = (bf16[1024,1024]{1,0:T(8,128)(2,1)S(1)}, bf16[1024,1024]{1,0:T(8,128)(2,1)}, u32[]{:S(2)}) copy-start(bf16[1024,1024]{1,0:T(8,128)(2,1)} %param.21) | copy-start | bytes 6291460
  4.5 4.9 %copy-start.1 = (s32[1,64]{1,0:T(1,128)S(1)}, s32[1,64]{1,0:T(1,128)}, u32[]{:S(2)}) copy-start(s32[1,64]{1,0:T(1,128)} %param.19) | copy-start | bytes 772
  7.8 0.8 copy-start.5
  8.6 10.2 %copy-start.2 = (bf16[2,96,1024]{2,1,0:T(8,128)(2,1)S(1)}, bf16[2,96,1024]{2,1,0:T(8,128)(2,1)}, u32[]{:S(2)}) copy-start(bf16[2,96,1024]{2,1,0:T(8,128)(2,1)} %param.16) | copy-start | bytes 1179652
  8.6 10.4 %copy-start.6 = (f32[1024]{0:T(1024)S(1)}, f32[1024]{0:T(1024)}, u32[]{:S(2)}) copy-start(f32[1024]{0:T(1024)} %param.22) | copy-start | bytes 12292
  11.5 17.9 %all-to-all-start.4 = ((bf16[8,4,2560]{2,1,0:T(4,128)(2,1)}), bf16[8,4,2560]{2,1,0:T(4,128)(2,1)}, u32[]{:S(2)}, u32[]{:S(2)}) async-start(bf16[8,4,2560]{2,1,0:T(4,128)(2,1)} %all_to_all.79), calls=%async_computation.4 | async-start | bytes 327680 | tf_op jit(solution)/shard_map/all_to_all | solution.py:141
  29.4 17.2 %all-to-all-start.1 = ((bf16[8,4,6144]{2,1,0:T(4,128)(2,1)}), bf16[8,4,6144]{2,1,0:T(4,128)(2,1)}, u32[]{:S(2)}, u32[]{:S(2)}) async-start(bf16[8,4,6144]{2,1,0:T(4,128)(2,1)} %all_to_all.71), calls=%async_computation.1 | async-start | bytes 786432 | tf_op jit(solution)/shard_map/all_to_all | solution.py:89
  37.4 18.7 %copy-start.8 = (s32[2]{0:T(128)S(1)}, s32[2]{0:T(128)}, u32[]{:S(2)}) copy-start(s32[2]{0:T(128)} %param.18) | copy-start | bytes 28
  46.6 15.3 %all-to-all-start.2 = ((bf16[8,4,6144]{2,1,0:T(4,128)(2,1)}), bf16[8,4,6144]{2,1,0:T(4,128)(2,1)}, u32[]{:S(2)}, u32[]{:S(2)}) async-start(bf16[8,4,6144]{2,1,0:T(4,128)(2,1)} %all_to_all.74), calls=%async_computation.2 | async-start | bytes 786432 | tf_op jit(solution)/shard_map/all_to_all | solution.py:90
  61.9 41.8 %all-to-all-start = ((bf16[8,4,6144]{2,1,0:T(4,128)(2,1)}), bf16[8,4,6144]{2,1,0:T(4,128)(2,1)}, u32[]{:S(2)}, u32[]{:S(2)}) async-start(bf16[8,4,6144]{2,1,0:T(4,128)(2,1)} %all_to_all.68), calls=%async_computation | async-start | bytes 786432 | tf_op jit(solution)/shard_map/all_to_all | solution.py:88
  103.7 67.2 %all-to-all-start.5 = ((bf16[4,8,2560]{2,0,1:T(4,128)(2,1)}), bf16[4,8,2560]{2,0,1:T(4,128)(2,1)}, u32[]{:S(2)}, u32[]{:S(2)}) async-start(bf16[4,8,2560]{2,0,1:T(4,128)(2,1)} %copy.76), calls=%async_computation.5 | async-start | bytes 327680 | tf_op jit(solution)/shard_map/all_to_all | solution.py:144
  170.8 15.8 %all-to-all-start.3 = ((bf16[4,8,6144]{2,0,1:T(4,128)(2,1)}), bf16[4,8,6144]{2,0,1:T(4,128)(2,1)S(1)}, u32[]{:S(2)}, u32[]{:S(2)}) async-start(bf16[4,8,6144]{2,0,1:T(4,128)(2,1)} %copy.71), calls=%async_computation.3 | async-start | bytes 786432 | tf_op jit(solution)/shard_map/all_to_all | solution.py:102
  176.8 2.9 %copy-start.7 = (f32[1024]{0:T(1024)S(1)}, f32[1024]{0:T(1024)}, u32[]{:S(2)}) copy-start(f32[1024]{0:T(1024)} %param.23) | copy-start | bytes 12292
  178.0 1.7 copy-start.4
  188.6 7.1 %copy-start.3 = (bf16[2,96,1024]{2,1,0:T(8,128)(2,1)S(1)}, bf16[2,96,1024]{2,1,0:T(8,128)(2,1)}, u32[]{:S(2)}) copy-start(bf16[2,96,1024]{2,1,0:T(8,128)(2,1)} %param.16) | copy-start | bytes 1179652
where the time goes:
time: 201 us; the launch traced here: 199 us
  local copies, waits for them, and re-layouts  74.7 us (37%)
  matrix products  37.3 us (19%)
  other arithmetic  36.8 us (18%)
  starting transfers between devices  33.5 us (17%)
  waiting for transfers between devices  14.4 us (7%)
    dot_general x12, matrix products, query_part(): jnp.dot(weights, values, preferred_element_type=jnp.float32)  15.2 us
    lt x20, other arithmetic, cand_part(): key_positions[None, :] < valid  12.7 us
    dynamic_slice x12, local copies, waits for them, and re-layouts, per_device(): lax.map(self_item, (heads_query, heads_keys, heads_values, item_valid))  8.53 us
    add x12, other arithmetic, query_part(): row_positions = first_row + jnp.arange(block_rows, dtype=jnp.int32)  8.29 us
    convert_element_type x3, local copies, waits for them, and re-layouts, per_device(): returned.astype(jnp.float32)  8.11 us
    dynamic_slice x12, local copies, waits for them, and re-layouts, self_item(): lax.map(query_part, (query.reshape(length // block_rows, block_rows, HD),...  7.94 us
    all_to_all x1, waiting for transfers between devices, per_device(): lax.all_to_all(to_items(keys), 'seq', split_axis=0, concat_axis=1, tiled=...  7.85 us
    squeeze x8, local copies, waits for them, and re-layouts, per_device(): lax.map(self_item, (heads_query, heads_keys, heads_values, item_valid))  7.62 us
  transfers between devices with their start and end apart: 6, of which 3 were waited for; matrix products, arithmetic and copies ran while one was open for 60% of the time, Pallas kernels for 0%

commit v1 on v0

--- a/solution.py
+++ b/solution.py
@@ -7,6 +7,22 @@
 H = 16
 HD = 64
 CAP = 40
+
+
+def pairwise_exchange(shard, axis, split, join):
+    ways, here = (lax.axis_size(axis), lax.axis_index(axis))
+    width = shard.shape[split] // ways
+    shape = list(shard.shape)
+    shape[split] = width
+    height = shape[join]
+    shape[join] = height * ways
+    full = jnp.zeros(shape, shard.dtype)
+    for mask in range(ways):
+        part = lax.dynamic_slice_in_dim(shard, (here ^ mask) * width, width, axis=split)
+        if mask:
+            part = lax.ppermute(part, axis, [(d, d ^ mask) for d in range(ways)])
+        full = lax.dynamic_update_slice_in_dim(full, part, (here ^ mask) * height, axis=join)
+    return full
 
 
 def rms_apply(values, gain):
@@ -99,9 +115,7 @@
         jnp.where(item_hist[:, None] == members[None, :], lengths[None, :], 0), axis=1
     )
     attended = lax.map(self_item, (heads_query, heads_keys, heads_values, item_valid))
-    returned = lax.all_to_all(
-        attended.reshape(items_local, length * HD), "seq", split_axis=1, concat_axis=0, tiled=True
-    )
+    returned = pairwise_exchange(attended.reshape(items_local, length * HD), "seq", 1, 0)
     returned = (
         returned.reshape(hist_local, H, tok_share, HD)
         .transpose(0, 2, 1, 3)

time: 201 us -> 224 us (1.11)
  local copies, waits for them, and re-layouts: 74.7 us -> 87 us
  waiting for transfers between devices: 14.4 us -> 19.4 us
  starting transfers between devices: 33.5 us -> 37.6 us
  other arithmetic: 36.8 us -> 39.6 us
    ppermute x0 -> x7, starting transfers between devices: none -> 12.6 us  [pairwise_exchange(): part = lax.ppermute(part, axis, [(d, d ^ mask) for d in range(ways)])]
    all_to_all x1, waiting for transfers between devices: 1.73 us -> 8.8 us  [per_device(): lax.all_to_all(to_items(values), 'seq', split_axis=0, concat_axis=1, tile...]
    dynamic_update_slice x0 -> x7, local copies, waits for them, and re-layouts: none -> 6.87 us  [pairwise_exchange(): lax.dynamic_update_slice_in_dim(full, part, (here ^ mask) * height, axis=...]
    all_to_all x1 -> x0, starting transfers between devices: 5.98 us -> none  [per_device(): lax.all_to_all(attended.reshape(items_local, length * HD), 'seq', split_a...]
    all_to_all x1 -> x0, waiting for transfers between devices: 4.8 us -> none  [per_device(): lax.all_to_all(attended.reshape(items_local, length * HD), 'seq', split_a...]
    all_to_all x2 -> x0, local copies, waits for them, and re-layouts: 2.82 us -> none  [per_device(): lax.all_to_all(attended.reshape(items_local, length * HD), 'seq', split_a...]
  transfers between devices with their start and end apart: 6 -> 12, of which waited for: 3 -> 4; matrix products, arithmetic and copies ran while one was open for 60% -> 36% of each run, Pallas kernels for 0% -> 0%
where the time goes in v1:
time: 224 us; the launch traced here: 222 us
  local copies, waits for them, and re-layouts  87 us (39%)
  other arithmetic  39.6 us (18%)
  starting transfers between devices  37.6 us (17%)
  matrix products  36.3 us (16%)
  waiting for transfers between devices  19.4 us (9%)
    dot_general x12, matrix products, query_part(): jnp.dot(weights, values, preferred_element_type=jnp.float32)  15.2 us
    lt x20, other arithmetic, cand_part(): key_positions[None, :] < valid  13.9 us
    ppermute x7, starting transfers between devices, pairwise_exchange(): part = lax.ppermute(part, axis, [(d, d ^ mask) for d in range(ways)])  12.6 us
    convert_element_type x3, local copies, waits for them, and re-layouts, per_device(): returned.astype(jnp.float32)  9.03 us
    dynamic_slice x12, local copies, waits for them, and re-layouts, per_device(): lax.map(self_item, (heads_query, heads_keys, heads_values, item_valid))  8.85 us
    all_to_all x1, waiting for transfers between devices, per_device(): lax.all_to_all(to_items(keys), 'seq', split_axis=0, concat_axis=1, tiled=...  8.84 us
    all_to_all x1, waiting for transfers between devices, per_device(): lax.all_to_all(to_items(values), 'seq', split_axis=0, concat_axis=1, tile...  8.8 us
    add x12, other arithmetic, query_part(): row_positions = first_row + jnp.arange(block_rows, dtype=jnp.int32)  8.1 us
  transfers between devices with their start and end apart: 12, of which 4 were waited for; matrix products, arithmetic and copies ran while one was open for 36% of the time, Pallas kernels for 0%

profile of v1, /device:TPU:0, one launch (start us, length us, event | category | flops | bytes accessed | tf_op | source)
XLA Modules:
  0.0 221.7 jit_solution(16595382955585027565)
XLA Ops:
  1.5 2.0 sort.31
  3.5 2.0 sort.32
  6.6 3.2 %fusion.37 = f32[64,2048]{1,0:T(8,128)S(1)} fusion(bf16[1024,4096]{1,0:T(8,128)(2,1)} %param.20, bf16[1,64,1024]{2,1,0:T(8,128)(2,1)} %param.17, f32[1024]{0:T(1024)} %param.22, f32[64]{0:T(128)S(1)} %add_rsqrt_fusion.3), kind=kOutput, calls=%fused_computation.50 | convolution fusion | flops 268697600 | bytes 4854016 | tf_op jit(solution)/shard_map/dot_general | solution.py:137
  13.5 7.3 %all-to-all-start.3 = ((bf16[8,4,2560]{2,1,0:T(4,128)(2,1)}), bf16[8,4,2560]{2,1,0:T(4,128)(2,1)}, u32[]{:S(2)}, u32[]{:S(2)}) async-start(bf16[8,4,2560]{2,1,0:T(4,128)(2,1)} %all_to_all.67), calls=%async_computation.3 | async-start | bytes 327680 | tf_op jit(solution)/shard_map/all_to_all | solution.py:155
  21.2 6.8 %fusion.61 = (bf16[192,4096]{1,0:T(8,128)(2,1)S(1)}, f32[192,4096]{1,0:T(8,128)}) fusion(bf16[192,1024]{1,0:T(8,128)(2,1)S(1)} %bitcast.137, bf16[1024,4096]{1,0:T(8,128)(2,1)} %param.20), kind=kOutput, calls=%fused_computation.126 | convolution fusion | flops 1611399168 | bytes 13500416 | tf_op jit(solution)/shard_map/dot_general | solution.py:90
  30.1 1.3 all_to_all.61
  31.4 6.0 %all-to-all-start.1 = ((bf16[8,4,6144]{2,1,0:T(4,128)(2,1)}), bf16[8,4,6144]{2,1,0:T(4,128)(2,1)}, u32[]{:S(2)}, u32[]{:S(2)}) async-start(bf16[8,4,6144]{2,1,0:T(4,128)(2,1)} %all_to_all.61), calls=%async_computation.1 | async-start | bytes 786432 | tf_op jit(solution)/shard_map/all_to_all | solution.py:105
  38.5 1.3 all_to_all.64
  39.7 8.8 %all-to-all-done.1 = bf16[8,4,6144]{2,1,0:T(4,128)(2,1)} async-done(((bf16[8,4,6144]{2,1,0:T(4,128)(2,1)}), bf16[8,4,6144]{2,1,0:T(4,128)(2,1)}, u32[]{:S(2)}, u32[]{:S(2)}) %all-to-all-start.1) | async-done | bytes 393248 | tf_op jit(solution)/shard_map/all_to_all | solution.py:105
  48.6 4.1 %all-to-all-start.2 = ((bf16[8,4,6144]{2,1,0:T(4,128)(2,1)}), bf16[8,4,6144]{2,1,0:T(4,128)(2,1)}, u32[]{:S(2)}, u32[]{:S(2)}) async-start(bf16[8,4,6144]{2,1,0:T(4,128)(2,1)} %all_to_all.64), calls=%async_computation.2 | async-start | bytes 786432 | tf_op jit(solution)/shard_map/all_to_all | solution.py:106
  53.8 1.3 all_to_all.58
  55.1 8.8 %all-to-all-done.2 = bf16[8,4,6144]{2,1,0:T(4,128)(2,1)} async-done(((bf16[8,4,6144]{2,1,0:T(4,128)(2,1)}), bf16[8,4,6144]{2,1,0:T(4,128)(2,1)}, u32[]{:S(2)}, u32[]{:S(2)}) %all-to-all-start.2) | async-done | bytes 393248 | tf_op jit(solution)/shard_map/all_to_all | solution.py:106
  63.9 3.6 %all-to-all-start = ((bf16[8,4,6144]{2,1,0:T(4,128)(2,1)}), bf16[8,4,6144]{2,1,0:T(4,128)(2,1)S(1)}, u32[]{:S(2)}, u32[]{:S(2)}) async-start(bf16[8,4,6144]{2,1,0:T(4,128)(2,1)} %all_to_all.58), calls=%async_computation | async-start | bytes 786432 | tf_op jit(solution)/shard_map/all_to_all | solution.py:104
  69.7 2.0 copy.64
  71.7 1.7 reshape.184
  73.4 2.0 copy.67
  75.4 2.6 %reshape.186 = bf16[4,768,64]{2,1,0:T(8,128)(2,1)} reshape(bf16[4,8,6144]{2,1,0:T(8,128)(2,1)} %copy.67) | data formatting | bytes 786432 | tf_op jit(solution)/shard_map/reshape | solution.py:110
  80.0 2.6 %reshape.182 = bf16[4,768,64]{2,1,0:T(8,128)(2,1)} reshape(bf16[4,8,6144]{2,1,0:T(8,128)(2,1)} %copy.61) | data formatting | bytes 786432 | tf_op jit(solution)/shard_map/reshape | solution.py:108
  82.6 55.9 %while.44 = (s32[]{:T(128)}, bf16[4,768,64]{2,1,0:T(8,128)(2,1)}, bf16[4,768,64]{2,1,0:T(8,128)(2,1)}, bf16[4,768,64]{2,1,0:T(8,128)(2,1)S(1)}, s32[4]{0:T(128)S...) while((s32[]{:T(128)}, bf16[4,768,64]{2,1,0:T(8,128)(2,1)}, ...), condition=%wide.region_5.6_spmd, body=%wide.region_2.5_spmd.sunk | while | flops 52118532 | bytes 1578542 | solution.py:117
  85.1 9.7 %while.47 = (s32[]{:T(128)}, bf16[3,256,64]{1,2,0:T(8,128)(2,1)}, s32[3]{0:T(128)S(1)}, s32[]{:T(128)}, bf16[3,256,64]{2,1,0:T(8,128)(2,1)S(1)}, /*index=5*/bf16...) while((s32[]{:T(128)}, bf16[3,256,64]{1,2,0:T(8,128)(2,1)}, ...), condition=%wide.region_4.4_spmd.clone.clone, body=%wide.region_3.3_spmd.clone.clone.sunk | while | flops 52118528 | bytes 496489 | solution.py:50
  87.1 1.3 fusion.85
  99.1 9.7 %while.47 = (s32[]{:T(128)}, bf16[3,256,64]{1,2,0:T(8,128)(2,1)}, s32[3]{0:T(128)S(1)}, s32[]{:T(128)}, bf16[3,256,64]{2,1,0:T(8,128)(2,1)S(1)}, /*index=5*/bf16...) while((s32[]{:T(128)}, bf16[3,256,64]{1,2,0:T(8,128)(2,1)}, ...), condition=%wide.region_4.4_spmd.clone.clone, body=%wide.region_3.3_spmd.clone.clone.sunk | while | flops 52118528 | bytes 496489 | solution.py:50
  101.1 1.3 fusion.85
  113.1 9.7 %while.47 = (s32[]{:T(128)}, bf16[3,256,64]{1,2,0:T(8,128)(2,1)}, s32[3]{0:T(128)S(1)}, s32[]{:T(128)}, bf16[3,256,64]{2,1,0:T(8,128)(2,1)S(1)}, /*index=5*/bf16...) while((s32[]{:T(128)}, bf16[3,256,64]{1,2,0:T(8,128)(2,1)}, ...), condition=%wide.region_4.4_spmd.clone.clone, body=%wide.region_3.3_spmd.clone.clone.sunk | while | flops 52118528 | bytes 496489 | solution.py:50
  118.3 1.3 fusion.85
  121.5 1.3 fusion.85
  127.1 9.7 %while.47 = (s32[]{:T(128)}, bf16[3,256,64]{1,2,0:T(8,128)(2,1)}, s32[3]{0:T(128)S(1)}, s32[]{:T(128)}, bf16[3,256,64]{2,1,0:T(8,128)(2,1)S(1)}, /*index=5*/bf16...) while((s32[]{:T(128)}, bf16[3,256,64]{1,2,0:T(8,128)(2,1)}, ...), condition=%wide.region_4.4_spmd.clone.clone, body=%wide.region_3.3_spmd.clone.clone.sunk | while | flops 52118528 | bytes 496489 | solution.py:50
  138.6 1.7 reshape.187
  141.8 1.4 collective-permute-start
  145.3 1.8 collective-permute-start.3
  147.1 2.0 collective-permute-start.4
  149.1 34.2 %while.46 = (s32[]{:T(128)}, bf16[4,320,64]{2,1,0:T(8,128)(2,1)}, bf16[4,320,64]{2,1,0:T(8,128)(2,1)}, bf16[4,768,64]{2,1,0:T(8,128)(2,1)S(1)}, s32[4]{0:T(128)S...) while((s32[]{:T(128)}, bf16[4,320,64]{2,1,0:T(8,128)(2,1)}, ...), condition=%wide.region_12.13_spmd, body=%wide.region_9.12_spmd.sunk | while | flops 12931844 | bytes 1027586 | solution.py:157
  151.6 5.4 %while.48 = (s32[]{:T(128)}, bf16[5,64,64]{2,1,0:T(8,128)(2,1)S(1)}, s32[]{:T(128)}, bf16[5,64,64]{2,1,0:T(8,128)(2,1)S(1)}, bf16[768,64]{1,0:T(8,128)(2,1)S(1)}, /*index=5*/bf16[768,64]{1,0:T(8,128)(2,1)S(1)}, s32[]{:T(128)}) while((s32[]{:T(128)}, bf16[5,64,64]{2,1,0:T(8,128)(2,1)S(1)}, s32[]{:T(128)}, ...), condition=%wide.region_11.11_spmd.clone, body=%wide.region_10.10_spmd.clone.sunk | while | flops 12931842 | bytes 428881 | solution.py:68
  160.2 5.4 %while.48 = (s32[]{:T(128)}, bf16[5,64,64]{2,1,0:T(8,128)(2,1)S(1)}, s32[]{:T(128)}, bf16[5,64,64]{2,1,0:T(8,128)(2,1)S(1)}, bf16[768,64]{1,0:T(8,128)(2,1)S(1)}, /*index=5*/bf16[768,64]{1,0:T(8,128)(2,1)S(1)}, s32[]{:T(128)}) while((s32[]{:T(128)}, bf16[5,64,64]{2,1,0:T(8,128)(2,1)S(1)}, s32[]{:T(128)}, ...), condition=%wide.region_11.11_spmd.clone, body=%wide.region_10.10_spmd.clone.sunk | while | flops 12931842 | bytes 428881 | solution.py:68
  168.7 5.4 %while.48 = (s32[]{:T(128)}, bf16[5,64,64]{2,1,0:T(8,128)(2,1)S(1)}, s32[]{:T(128)}, bf16[5,64,64]{2,1,0:T(8,128)(2,1)S(1)}, bf16[768,64]{1,0:T(8,128)(2,1)S(1)}, /*index=5*/bf16[768,64]{1,0:T(8,128)(2,1)S(1)}, s32[]{:T(128)}) while((s32[]{:T(128)}, bf16[5,64,64]{2,1,0:T(8,128)(2,1)S(1)}, s32[]{:T(128)}, ...), condition=%wide.region_11.11_spmd.clone, body=%wide.region_10.10_spmd.clone.sunk | while | flops 12931842 | bytes 428881 | solution.py:68
  177.3 5.4 %while.48 = (s32[]{:T(128)}, bf16[5,64,64]{2,1,0:T(8,128)(2,1)S(1)}, s32[]{:T(128)}, bf16[5,64,64]{2,1,0:T(8,128)(2,1)S(1)}, bf16[768,64]{1,0:T(8,128)(2,1)S(1)}, /*index=5*/bf16[768,64]{1,0:T(8,128)(2,1)S(1)}, s32[]{:T(128)}) while((s32[]{:T(128)}, bf16[5,64,64]{2,1,0:T(8,128)(2,1)S(1)}, s32[]{:T(128)}, ...), condition=%wide.region_11.11_spmd.clone, body=%wide.region_10.10_spmd.clone.sunk | while | flops 12931842 | bytes 428881 | solution.py:68
  185.3 4.0 %all-to-all-start.4 = ((bf16[4,8,2560]{2,0,1:T(4,128)(2,1)}), bf16[4,8,2560]{2,0,1:T(4,128)(2,1)S(1)}, u32[]{:S(2)}, u32[]{:S(2)}) async-start(bf16[4,8,2560]{2,0,1:T(4,128)(2,1)} %copy.72), calls=%async_computation.4 | async-start | bytes 327680 | tf_op jit(solution)/shard_map/all_to_all | solution.py:158
  189.3 3.8 %collective-permute-start.5 = (bf16[4,6144]{1,0:T(4,128)(2,1)}, bf16[4,6144]{1,0:T(4,128)(2,1)S(1)}, u32[]{:S(2)}, u32[]{:S(2)}) collective-permute-start(bf16[4,6144]{1,0:T(4,128)(2,1)} %get-tuple-element.264), channel_id=1, source_target_pairs={{0,6},{1,7},{2,4},{3,5},{4,2},{5,3},{6,0},{7,1},{8,14},{9,15},{10,... | collective-permute-start | bytes 147464 | tf_op jit(solution)/shard_map/ppermute | solution.py:23
  193.1 1.4 constant_dynamic-update-slice_fusion.6
  194.5 1.5 collective-permute-start.6
  196.0 1.4 constant_dynamic-update-slice_fusion.5
  197.4 1.4 constant_dynamic-update-slice_fusion.4
  202.2 2.9 %reshape.195 = f32[2,16,96,64]{3,2,1,0:T(8,128)} reshape(bf16[32,6144]{1,0:T(8,128)(2,1)} %constant_dynamic-update-slice_fusion) | data formatting | bytes 1179648 | tf_op jit(solution)/shard_map/convert_element_type | solution.py:125
  206.1 3.5 %copy.74 = f32[2,96,16,64]{3,2,1,0:T(8,128)} copy(f32[2,96,16,64]{3,1,2,0:T(8,128)} %bitcast.134) | data formatting | bytes 1572864 | tf_op jit(solution)/shard_map/convert_element_type | solution.py:125
  209.6 2.7 %reshape.223 = f32[192,1024]{1,0:T(8,128)} reshape(f32[2,96,16,64]{3,2,1,0:T(8,128)} %copy.74) | data formatting | bytes 1572864 | tf_op jit(solution)/shard_map/convert_element_type | solution.py:125
  212.3 1.8 mul.187
  214.0 1.6 reduce_sum.47
  215.8 2.8 %fusion.39 = bf16[192,1024]{1,0:T(8,128)(2,1)} fusion(bf16[1024,1024]{1,0:T(8,128)(2,1)S(1)} %copy-done, f32[192,1024]{1,0:T(8,128)} %reshape.223, f32[192,4096]{1,0:T(8,128)} %get-tuple-element.276, f32[1024]{0:T(1024)S(1)} %copy-done.10, f32[192]{0:T(256)S(1)} %rsqrt.37, bf16[192,1024]{1,0:T(8,128)(2,1)S(1)} %bitcast.143), kind=kOutput, calls=%fused_computation.53 | convolution fusion | flops 405209088 | bytes 4461312 | tf_op jit(solution)/shard_map/dot_general | solution.py:127
  (226 shorter events, 111.5 us)
Async XLA Ops:
  0.6 215.1 %copy-start = (bf16[1024,1024]{1,0:T(8,128)(2,1)S(1)}, bf16[1024,1024]{1,0:T(8,128)(2,1)}, u32[]{:S(2)}) copy-start(bf16[1024,1024]{1,0:T(8,128)(2,1)} %param.21) | copy-start | bytes 6291460
  6.6 4.9 %copy-start.1 = (s32[1,64]{1,0:T(1,128)S(1)}, s32[1,64]{1,0:T(1,128)}, u32[]{:S(2)}) copy-start(s32[1,64]{1,0:T(1,128)} %param.19) | copy-start | bytes 772
  9.8 0.8 copy-start.7
  10.6 10.2 %copy-start.4 = (bf16[2,96,1024]{2,1,0:T(8,128)(2,1)S(1)}, bf16[2,96,1024]{2,1,0:T(8,128)(2,1)}, u32[]{:S(2)}) copy-start(bf16[2,96,1024]{2,1,0:T(8,128)(2,1)} %param.16) | copy-start | bytes 1179652
  10.8 10.2 %copy-start.9 = (f32[1024]{0:T(1024)S(1)}, f32[1024]{0:T(1024)}, u32[]{:S(2)}) copy-start(f32[1024]{0:T(1024)} %param.22) | copy-start | bytes 12292
  13.5 17.8 %all-to-all-start.3 = ((bf16[8,4,2560]{2,1,0:T(4,128)(2,1)}), bf16[8,4,2560]{2,1,0:T(4,128)(2,1)}, u32[]{:S(2)}, u32[]{:S(2)}) async-start(bf16[8,4,2560]{2,1,0:T(4,128)(2,1)} %all_to_all.67), calls=%async_computation.3 | async-start | bytes 327680 | tf_op jit(solution)/shard_map/all_to_all | solution.py:155
  30.1 7.3 %copy-start.3 = (bf16[192,1024]{1,0:T(8,128)(2,1)S(1)}, bf16[192,1024]{1,0:T(8,128)(2,1)}, u32[]{:S(2)}) copy-start(bf16[192,1024]{1,0:T(8,128)(2,1)} %get-tuple-element.258) | copy-start | bytes 1179652
  31.4 17.2 %all-to-all-start.1 = ((bf16[8,4,6144]{2,1,0:T(4,128)(2,1)}), bf16[8,4,6144]{2,1,0:T(4,128)(2,1)}, u32[]{:S(2)}, u32[]{:S(2)}) async-start(bf16[8,4,6144]{2,1,0:T(4,128)(2,1)} %all_to_all.61), calls=%async_computation.1 | async-start | bytes 786432 | tf_op jit(solution)/shard_map/all_to_all | solution.py:105
  38.4 14.2 %copy-start.2 = (bf16[192,1024]{1,0:T(8,128)(2,1)S(1)}, bf16[192,1024]{1,0:T(8,128)(2,1)}, u32[]{:S(2)}) copy-start(bf16[192,1024]{1,0:T(8,128)(2,1)} %get-tuple-element.260) | copy-start | bytes 1179652
  48.6 15.3 %all-to-all-start.2 = ((bf16[8,4,6144]{2,1,0:T(4,128)(2,1)}), bf16[8,4,6144]{2,1,0:T(4,128)(2,1)}, u32[]{:S(2)}, u32[]{:S(2)}) async-start(bf16[8,4,6144]{2,1,0:T(4,128)(2,1)} %all_to_all.64), calls=%async_computation.2 | async-start | bytes 786432 | tf_op jit(solution)/shard_map/all_to_all | solution.py:106
  52.9 14.8 %copy-start.11 = (s32[2]{0:T(128)S(1)}, s32[2]{0:T(128)}, u32[]{:S(2)}) copy-start(s32[2]{0:T(128)} %param.18) | copy-start | bytes 28
  63.9 15.2 %all-to-all-start = ((bf16[8,4,6144]{2,1,0:T(4,128)(2,1)}), bf16[8,4,6144]{2,1,0:T(4,128)(2,1)S(1)}, u32[]{:S(2)}, u32[]{:S(2)}) async-start(bf16[8,4,6144]{2,1,0:T(4,128)(2,1)} %all_to_all.58), calls=%async_computation | async-start | bytes 786432 | tf_op jit(solution)/shard_map/all_to_all | solution.py:104
  141.8 47.4 %collective-permute-start = (bf16[4,6144]{1,0:T(4,128)(2,1)}, bf16[4,6144]{1,0:T(4,128)(2,1)}, u32[]{:S(2)}, u32[]{:S(2)}) collective-permute-start(bf16[4,6144]{1,0:T(4,128)(2,1)} %get-tuple-element.269), channel_id=1, source_target_pairs={{0,1},{1,0},{2,3},{3,2},{4,5},{5,4},{6,7},{7,6},{8,9},{9,8},{10,11... | collective-permute-start | bytes 147464 | tf_op jit(solution)/shard_map/ppermute | solution.py:23
  143.3 51.3 %collective-permute-start.1 = (bf16[4,6144]{1,0:T(4,128)(2,1)}, bf16[4,6144]{1,0:T(4,128)(2,1)}, u32[]{:S(2)}, u32[]{:S(2)}) collective-permute-start(bf16[4,6144]{1,0:T(4,128)(2,1)} %get-tuple-element.268), channel_id=1, source_target_pairs={{0,2},{1,3},{2,0},{3,1},{4,6},{5,7},{6,4},{7,5},{8,10},{9,11},{10,... | collective-permute-start | bytes 147464 | tf_op jit(solution)/shard_map/ppermute | solution.py:23
  144.2 53.3 %collective-permute-start.2 = (bf16[4,6144]{1,0:T(4,128)(2,1)}, bf16[4,6144]{1,0:T(4,128)(2,1)}, u32[]{:S(2)}, u32[]{:S(2)}) collective-permute-start(bf16[4,6144]{1,0:T(4,128)(2,1)} %get-tuple-element.267), channel_id=1, source_target_pairs={{0,3},{1,2},{2,1},{3,0},{4,7},{5,6},{6,5},{7,4},{8,11},{9,10},{10,... | collective-permute-start | bytes 147464 | tf_op jit(solution)/shard_map/ppermute | solution.py:23
  145.3 53.6 %collective-permute-start.3 = (bf16[4,6144]{1,0:T(4,128)(2,1)}, bf16[4,6144]{1,0:T(4,128)(2,1)S(1)}, u32[]{:S(2)}, u32[]{:S(2)}) collective-permute-start(bf16[4,6144]{1,0:T(4,128)(2,1)} %get-tuple-element.266), channel_id=1, source_target_pairs={{0,4},{1,5},{2,6},{3,7},{4,0},{5,1},{6,2},{7,3},{8,12},{9,13},{10,... | collective-permute-start | bytes 147464 | tf_op jit(solution)/shard_map/ppermute | solution.py:23
  147.1 52.4 %collective-permute-start.4 = (bf16[4,6144]{1,0:T(4,128)(2,1)}, bf16[4,6144]{1,0:T(4,128)(2,1)S(1)}, u32[]{:S(2)}, u32[]{:S(2)}) collective-permute-start(bf16[4,6144]{1,0:T(4,128)(2,1)} %get-tuple-element.265), channel_id=1, source_target_pairs={{0,5},{1,4},{2,7},{3,6},{4,1},{5,0},{6,3},{7,2},{8,13},{9,12},{10,... | collective-permute-start | bytes 147464 | tf_op jit(solution)/shard_map/ppermute | solution.py:23
  185.3 33.3 %all-to-all-start.4 = ((bf16[4,8,2560]{2,0,1:T(4,128)(2,1)}), bf16[4,8,2560]{2,0,1:T(4,128)(2,1)S(1)}, u32[]{:S(2)}, u32[]{:S(2)}) async-start(bf16[4,8,2560]{2,0,1:T(4,128)(2,1)} %copy.72), calls=%async_computation.4 | async-start | bytes 327680 | tf_op jit(solution)/shard_map/all_to_all | solution.py:158
  189.3 10.9 %collective-permute-start.5 = (bf16[4,6144]{1,0:T(4,128)(2,1)}, bf16[4,6144]{1,0:T(4,128)(2,1)S(1)}, u32[]{:S(2)}, u32[]{:S(2)}) collective-permute-start(bf16[4,6144]{1,0:T(4,128)(2,1)} %get-tuple-element.264), channel_id=1, source_target_pairs={{0,6},{1,7},{2,4},{3,5},{4,2},{5,3},{6,0},{7,1},{8,14},{9,15},{10,... | collective-permute-start | bytes 147464 | tf_op jit(solution)/shard_map/ppermute | solution.py:23
  194.5 7.0 %collective-permute-start.6 = (bf16[4,6144]{1,0:T(4,128)(2,1)}, bf16[4,6144]{1,0:T(4,128)(2,1)S(1)}, u32[]{:S(2)}, u32[]{:S(2)}) collective-permute-start(bf16[4,6144]{1,0:T(4,128)(2,1)} %get-tuple-element.263), channel_id=1, source_target_pairs={{0,7},{1,6},{2,5},{3,4},{4,3},{5,2},{6,1},{7,0},{8,15},{9,14},{10,... | collective-permute-start | bytes 147464 | tf_op jit(solution)/shard_map/ppermute | solution.py:23
  212.3 3.5 %copy-start.5 = (bf16[2,96,1024]{2,1,0:T(8,128)(2,1)S(1)}, bf16[2,96,1024]{2,1,0:T(8,128)(2,1)}, u32[]{:S(2)}) copy-start(bf16[2,96,1024]{2,1,0:T(8,128)(2,1)} %param.16) | copy-start | bytes 1179652
  212.3 3.5 %copy-start.10 = (f32[1024]{0:T(1024)S(1)}, f32[1024]{0:T(1024)}, u32[]{:S(2)}) copy-start(f32[1024]{0:T(1024)} %param.23) | copy-start | bytes 12292
  219.0 1.5 copy-start.6
  219.0 1.5 copy-start.8
